TPU v7x, 32 devices: a 4x2x2 block of a 4x4x8 slice. The times are simulated.
32 devices in a mesh: dp: 4 (over y, z), cp: 8 (over x, core).
Axes of the slice: x: 4, y: 2, z: 2, core: 2. Of those that a mesh axis runs over, the one named last changes fastest.
The devices are a block of a 4x4x8 slice.
Arguments:
- vis_feat: bfloat16 [32, 4096, 1152], P(('dp', 'cp')), parts along dimension 0
- text_emb: bfloat16 [16384, 2048], P(('dp', 'cp')), parts along dimension 0
- img_pos: int32 [32], P('dp'), parts along dimension 0
- grad_y: bfloat16 [16384, 2048], P(('dp', 'cp')), parts along dimension 0
- pn_gain: bfloat16 [1152], replicated
- w_proj: bfloat16 [1152, 2048], replicated
- pre_gain: bfloat16 [2048], replicated
- w_query: bfloat16 [2048, 2048], replicated
- w_key: bfloat16 [2048, 256], replicated
- w_value: bfloat16 [2048, 256], replicated
- q_gain: bfloat16 [256], replicated
- k_gain: bfloat16 [256], replicated
- w_out: bfloat16 [2048, 2048], replicated
- post_gain: bfloat16 [2048], replicated
Outputs:
- output 1: bfloat16 [16384, 2048], P(('dp', 'cp')), parts along dimension 0
- output 2: bfloat16 [16384, 2048], P(('dp', 'cp')), parts along dimension 0
- output 3: bfloat16 [32, 4096, 1152], P(('dp', 'cp')), parts along dimension 0
- output 4: bfloat16 [4608], P('dp'), parts along dimension 0
- output 5: bfloat16 [4608, 2048], P('dp'), parts along dimension 0
- output 6: bfloat16 [8192], P('dp'), parts along dimension 0
- output 7: bfloat16 [8192, 2048], P('dp'), parts along dimension 0
- output 8: bfloat16 [8192, 256], P('dp'), parts along dimension 0
- output 9: bfloat16 [8192, 256], P('dp'), parts along dimension 0
- output 10: bfloat16 [1024], P('dp'), parts along dimension 0
- output 11: bfloat16 [1024], P('dp'), parts along dimension 0
- output 12: bfloat16 [8192, 2048], P('dp'), parts along dimension 0
- output 13: bfloat16 [8192], P('dp'), parts along dimension 0
There are 4 independent parts. A program takes and returns all parts, laid end to end along the dimension named above; an argument that names none is the same for every part.
All inputs are finite; a program needn't handle non-finite values.
Results may differ from a plain program's by a relative error of at most 0.02.
Values are sent between devices in bfloat16 or wider.
A program may use at most 768 MiB of HBM per device.

v0:
```python
import functools
import jax
import jax.numpy as jnp
from jax import lax
from jax.sharding import PartitionSpec as P

GRID = 64
POOL = 4
EPS = 1e-6
ROPE_BASE = 1000000.0
ROPE_SCALE = 8.0
NEG_BIG = -1e30


def rms_scale(values, gain_vec):
    wide_vals = values.astype(jnp.float32)
    mean_sq = jnp.mean(wide_vals * wide_vals, axis=-1, keepdims=True)
    return wide_vals * lax.rsqrt(mean_sq + EPS) * (1.0 + gain_vec)


def gain_norm(values, gain_vec):
    return rms_scale(values, gain_vec).astype(jnp.bfloat16)


def rope_tables(positions, head_dim):
    inv_freq = ROPE_BASE ** (-jnp.arange(0, head_dim, 2).astype(jnp.float32) / head_dim)
    rot_angle = (positions.astype(jnp.float32) / ROPE_SCALE)[:, None] * inv_freq[None, :]
    rot_angle = jnp.concatenate([rot_angle, rot_angle], axis=-1)
    return jnp.cos(rot_angle)[:, None, :], jnp.sin(rot_angle)[:, None, :]


def apply_rope(values, cos_t, sin_t):
    half_dim = values.shape[-1] // 2
    rotated = jnp.concatenate([-values[..., half_dim:], values[..., :half_dim]], axis=-1)
    return values * cos_t + rotated * sin_t


def qk_rotate(q_raw, k_raw, q_gain, k_gain, cos_t, sin_t):
    q_heads = apply_rope(rms_scale(q_raw, q_gain), cos_t, sin_t).astype(jnp.bfloat16)
    k_heads = apply_rope(rms_scale(k_raw, k_gain), cos_t, sin_t).astype(jnp.bfloat16)
    return q_heads, k_heads


def post_residual(merged, proj_out, gain_vec):
    return (merged.astype(jnp.float32) + rms_scale(proj_out, gain_vec)).astype(jnp.bfloat16)


def pool_patches(vis_loc):
    img_count = vis_loc.shape[0]
    dim_v = vis_loc.shape[2]
    side_len = GRID // POOL
    patch_grid = vis_loc.reshape(img_count, side_len, POOL, side_len, POOL, dim_v)
    pooled = jnp.sum(patch_grid, axis=(2, 4), dtype=jnp.float32) / (POOL * POOL)
    return pooled.astype(jnp.bfloat16).reshape(img_count * side_len * side_len, dim_v)


def unpool_grad(d_pooled, img_count):
    side_len = GRID // POOL
    dim_v = d_pooled.shape[-1]
    spread = (d_pooled.astype(jnp.float32) / (POOL * POOL)).reshape(img_count, side_len, 1, side_len, 1, dim_v)
    spread = jnp.broadcast_to(spread, (img_count, side_len, POOL, side_len, POOL, dim_v))
    return spread.astype(jnp.bfloat16).reshape(img_count, GRID * GRID, dim_v)


def merge_layout(img_pos, dev_rank, seq_loc, block_len):
    q_pos = dev_rank * seq_loc + jnp.arange(seq_loc)
    offset = q_pos[:, None] - img_pos[None, :]
    in_blk = (offset >= 0) & (offset < block_len)
    is_img = jnp.any(in_blk, axis=1)
    flat_row = jnp.sum(jnp.where(in_blk, jnp.arange(img_pos.shape[0])[None, :] * block_len + offset, 0), axis=1)
    blk_start = jnp.where(is_img, q_pos - jnp.sum(jnp.where(in_blk, offset, 0), axis=1), -block_len)
    return q_pos, is_img, flat_row, blk_start


def attn_forward(q_heads, k_all, v_all, visible):
    seq_loc = q_heads.shape[0]
    head_dim = q_heads.shape[-1]
    q_grp = q_heads.reshape(seq_loc, k_all.shape[1], -1, head_dim)
    scores = jnp.einsum('qkgd,skd->kgqs', q_grp, k_all, preferred_element_type=jnp.float32) * head_dim ** -0.5
    probs_hi = jax.nn.softmax(jnp.where(visible, scores, NEG_BIG), axis=-1)
    probs_lo = probs_hi.astype(jnp.bfloat16)
    attn_out = jnp.einsum('kgqs,skd->qkgd', probs_lo, v_all, preferred_element_type=jnp.float32)
    return attn_out.astype(jnp.bfloat16).reshape(seq_loc, -1), probs_hi, probs_lo


def attn_backward(d_attn, q_heads, k_all, v_all, probs_hi, probs_lo):
    seq_loc = q_heads.shape[0]
    head_dim = q_heads.shape[-1]
    q_grp = q_heads.reshape(seq_loc, k_all.shape[1], -1, head_dim)
    d_grp = d_attn.reshape(q_grp.shape)
    d_probs = jnp.einsum('qkgd,skd->kgqs', d_grp, v_all, preferred_element_type=jnp.float32)
    d_v_part = jnp.einsum('kgqs,qkgd->skd', probs_lo, d_grp, preferred_element_type=jnp.float32)
    d_scores = probs_hi * (d_probs - jnp.sum(d_probs * probs_hi, axis=-1, keepdims=True)) * head_dim ** -0.5
    d_scores = d_scores.astype(jnp.bfloat16)
    d_q = jnp.einsum('kgqs,skd->qkgd', d_scores, k_all, preferred_element_type=jnp.float32).astype(jnp.bfloat16).reshape(q_heads.shape)
    d_k_part = jnp.einsum('kgqs,qkgd->skd', d_scores, q_grp, preferred_element_type=jnp.float32)
    return d_q, d_k_part, d_v_part


def solution(mesh):
    group_size = mesh.shape['cp']
    seq_spec = P(('dp', 'cp'))
    part_spec = P('dp')
    rep_spec = P()

    def device_body(vis_loc, text_loc, img_pos, grad_y, pn_gain, w_proj, pre_gain, w_query, w_key, w_value, q_gain, k_gain, w_out, post_gain):
        dev_rank = lax.axis_index('cp')
        seq_loc = text_loc.shape[0]
        img_loc = vis_loc.shape[0]
        head_dim = q_gain.shape[0]
        block_len = (GRID // POOL) ** 2
        pooled = pool_patches(vis_loc)
        normed, norm_pull = jax.vjp(gain_norm, pooled, pn_gain.astype(jnp.float32))
        soft_loc = jnp.dot(normed, w_proj, preferred_element_type=jnp.float32).astype(jnp.bfloat16)
        soft_all = lax.all_gather(soft_loc, 'cp', tiled=True)
        q_pos, is_img, flat_row, blk_start = merge_layout(img_pos, dev_rank, seq_loc, block_len)
        img_mask = is_img[:, None]
        merged = jnp.where(img_mask, jnp.take(soft_all, flat_row, axis=0), text_loc)
        hidden, pre_pull = jax.vjp(gain_norm, merged, pre_gain.astype(jnp.float32))
        q_raw = jnp.dot(hidden, w_query, preferred_element_type=jnp.float32).astype(jnp.bfloat16).reshape(seq_loc, -1, head_dim)
        k_raw = jnp.dot(hidden, w_key, preferred_element_type=jnp.float32).astype(jnp.bfloat16).reshape(seq_loc, -1, head_dim)
        v_loc = jnp.dot(hidden, w_value, preferred_element_type=jnp.float32).astype(jnp.bfloat16).reshape(seq_loc, -1, head_dim)
        cos_t, sin_t = rope_tables(q_pos, head_dim)
        rotate_fn = functools.partial(qk_rotate, cos_t=cos_t, sin_t=sin_t)
        (q_heads, k_loc), qk_pull = jax.vjp(rotate_fn, q_raw, k_raw, q_gain.astype(jnp.float32), k_gain.astype(jnp.float32))
        k_all = lax.all_gather(k_loc, 'cp', tiled=True)
        v_all = lax.all_gather(v_loc, 'cp', tiled=True)
        key_pos = jnp.arange(seq_loc * group_size)
        visible = (key_pos[None, :] <= q_pos[:, None]) | ((key_pos[None, :] >= blk_start[:, None]) & (key_pos[None, :] < blk_start[:, None] + block_len))
        attn_out, probs_hi, probs_lo = attn_forward(q_heads, k_all, v_all, visible)
        proj_out = jnp.dot(attn_out, w_out, preferred_element_type=jnp.float32).astype(jnp.bfloat16)
        y_loc, post_pull = jax.vjp(post_residual, merged, proj_out, post_gain.astype(jnp.float32))
        d_resid, d_proj, g_post = post_pull(grad_y)
        g_out = jnp.einsum('sh,sd->hd', attn_out, d_proj, preferred_element_type=jnp.float32)
        d_attn = jnp.einsum('sd,hd->sh', d_proj, w_out, preferred_element_type=jnp.float32).astype(jnp.bfloat16)
        d_q, d_k_part, d_v_part = attn_backward(d_attn, q_heads, k_all, v_all, probs_hi, probs_lo)
        d_k_loc = lax.psum_scatter(d_k_part, 'cp', scatter_dimension=0, tiled=True).astype(jnp.bfloat16)
        d_v_loc = lax.psum_scatter(d_v_part, 'cp', scatter_dimension=0, tiled=True).astype(jnp.bfloat16)
        d_q_raw, d_k_raw, g_q_gain, g_k_gain = qk_pull((d_q, d_k_loc))
        d_q_flat = d_q_raw.reshape(seq_loc, -1)
        d_k_flat = d_k_raw.reshape(seq_loc, -1)
        d_v_flat = d_v_loc.reshape(seq_loc, -1)
        d_hidden = jnp.einsum('sh,dh->sd', d_q_flat, w_query, preferred_element_type=jnp.float32)
        d_hidden = d_hidden + jnp.einsum('sh,dh->sd', d_k_flat, w_key, preferred_element_type=jnp.float32)
        d_hidden = (d_hidden + jnp.einsum('sh,dh->sd', d_v_flat, w_value, preferred_element_type=jnp.float32)).astype(jnp.bfloat16)
        g_query = jnp.einsum('sd,sh->dh', hidden, d_q_flat, preferred_element_type=jnp.float32)
        g_key = jnp.einsum('sd,sh->dh', hidden, d_k_flat, preferred_element_type=jnp.float32)
        g_value = jnp.einsum('sd,sh->dh', hidden, d_v_flat, preferred_element_type=jnp.float32)
        d_merged_attn, g_pre = pre_pull(d_hidden)
        d_merged = (d_resid.astype(jnp.float32) + d_merged_attn.astype(jnp.float32)).astype(jnp.bfloat16)
        grad_text = jnp.where(img_mask, 0.0, d_merged).astype(jnp.bfloat16)
        d_soft_all = jnp.zeros_like(soft_all).at[flat_row].add(jnp.where(img_mask, d_merged, 0.0).astype(jnp.bfloat16))
        d_soft_loc = lax.psum_scatter(d_soft_all, 'cp', scatter_dimension=0, tiled=True)
        g_proj = jnp.einsum('nc,nd->cd', normed, d_soft_loc, preferred_element_type=jnp.float32)
        d_normed = jnp.einsum('nd,cd->nc', d_soft_loc, w_proj, preferred_element_type=jnp.float32).astype(jnp.bfloat16)
        d_pooled, g_pn = norm_pull(d_normed)
        grad_vis = unpool_grad(d_pooled, img_loc)
        weight_grads = lax.psum((g_pn, g_proj, g_pre, g_query, g_key, g_value, g_q_gain, g_k_gain, g_out, g_post), 'cp')
        return (y_loc, grad_text, grad_vis) + tuple(grad_part.astype(jnp.bfloat16) for grad_part in weight_grads)

    in_specs = (seq_spec, seq_spec, part_spec, seq_spec) + (rep_spec,) * 10
    out_specs = (seq_spec, seq_spec, seq_spec) + (part_spec,) * 10
    return jax.shard_map(device_body, mesh=mesh, in_specs=in_specs, out_specs=out_specs, check_vma=False)
```

profile of v0, /device:TPU:87, one launch (start us, length us, event | category | flops | bytes accessed | tf_op | source)
XLA Modules:
  0.0 1110.0 jit_solution(14637915232943190919)
XLA Ops:
  7.3 17.9 %reshape.499 = f32[16,4,16,4,1152]{4,3,2,1,0:T(4,128)} reshape(bf16[1,4096,1152]{2,1,0:T(8,128)(2,1)} %param.14) | data formatting | bytes 28311552 | tf_op jit(solution)/shard_map/convert_element_type | solution.py:53
  25.2 11.6 %reduce_sum.181 = f32[16,16,1152]{2,1,0:T(8,128)S(1)} reduce(f32[16,4,16,4,1152]{4,3,2,1,0:T(4,128)} %reshape.499, f32[]{:T(128)} %constant.30.clone.1), dimensions={1,3}, to_apply=%region_2.0 | reduce | flops 4423680 | bytes 20054020 | tf_op jit(solution)/shard_map/reduce_sum | solution.py:53
  47.4 43.9 %all-gather.6.cloned.1.call-done = bf16[2048,2048]{1,0:T(8,128)(2,1)} async-done(((bf16[256,2048]{1,0:T(8,128)(2,1)}), bf16[2048,2048]{1,0:T(8,128)(2,1)}) %all-gather.6.cloned.1.call-update) | async-done | bytes 8388624 | tf_op jit(solution)/shard_map/all_gather | solution.py:115
  91.2 9.7 gather_fusion
  109.6 7.7 fusion.30
  121.4 5.2 copy.112
  137.1 5.3 copy.133
  146.1 5.4 copy.132
  154.0 5.4 copy.131
  162.7 9.1 add_convert_fusion.2
  171.8 27.7 %fusion.6 = (f32[8,512]{1,0:T(8,128)S(1)}, f32[4096,512,8]{1,0,2:T(8,128)}) fusion(pred[512,4096]{0,1:T(8,128)(4,1)S(1)} %fusion.8, bf16[64,8,8,256]{3,2,1,0:T(8,128)(2,1)} %bitcast.202, bf16[4096,256]{0,1:T(8,128)(2,1)} %all-gather.10.cloned.1.call-done), kind=kOutput, calls=%fused_computation.12 | convolution fusion | flops 8640262144 | bytes 73416704 | tf_op jit(solution)/shard_map/qkgd,skd->kgqs/dot_general | solution.py:79
  199.5 21.5 %fusion.5 = f32[8,512]{1,0:T(8,128)S(1)} fusion(f32[4096,512,8]{1,0,2:T(8,128)} %get-tuple-element.61, f32[8,512]{1,0:T(8,128)S(1)} %get-tuple-element.60, pred[512,4096]{0,1:T(8,128)(4,1)S(1)} %fusion.8), kind=kLoop, calls=%fused_computation.11 | loop fusion | flops 67104768 | bytes 69238784 | tf_op jit(solution)/shard_map/reduce_sum | solution.py:80
  221.1 33.7 %convert_bitcast_fusion = bf16[8,512,4096]{1,2,0:T(8,128)(2,1)} fusion(f32[8,512]{1,0:T(8,128)S(1)} %fusion.5, f32[8,512]{1,0:T(8,128)S(1)} %get-tuple-element.60, f32[4096,512,8]{1,0,2:T(8,128)} %get-tuple-element.61, pred[512,4096]{0,1:T(8,128)(4,1)S(1)} %fusion.8), kind=kLoop, calls=%fused_computation.14 | loop fusion | flops 83886080 | bytes 102793216 | tf_op jit(solution)/shard_map/reshape.9
  254.8 15.7 %fusion.47 = bf16[256,8,512]{2,0,1:T(8,128)(2,1)S(1)} fusion(bf16[8,512,4096]{1,2,0:T(8,128)(2,1)} %convert_bitcast_fusion, bf16[4096,256]{1,0:T(8,128)(2,1)} %all-gather.8.cloned.1.call-done), kind=kOutput, calls=%fused_computation.95 | convolution fusion | flops 8590983168 | bytes 37748736 | tf_op jit(solution)/shard_map/kgqs,skd->qkgd/dot_general | solution.py:82
  270.5 9.2 fusion.21
  283.9 9.7 convolution_convert_fusion
  293.6 52.7 %fusion = (f32[8,512]{1,0:T(8,128)S(1)}, f32[4096,512,8]{1,0,2:T(8,128)}) fusion(f32[8,512]{1,0:T(8,128)S(1)} %fusion.5, f32[8,512]{1,0:T(8,128)S(1)} %get-tuple-element.60, f32[4096,512,8]{1,0,2:T(8,128)} %get-tuple-element.61, pred[512,4096]{0,1:T(8,128)(4,1)S(1)} %fusion.8, bf16[64,8,8,256]{3,2,1,0:T(8,128)(2,1)} %bitcast.203, ...), kind=kOutput, calls=%fused_computation.5 | convolution fusion | flops 8690593792 | bytes 140558336 | tf_op jit(solution)/shard_map/qkgd,skd->kgqs/dot_general | solution.py:91
  346.3 53.5 %fusion.7 = bf16[8,512,4096]{1,2,0:T(8,128)(2,1)} fusion(f32[4096,512,8]{1,0,2:T(8,128)} %get-tuple-element.65, f32[8,512]{1,0:T(8,128)S(1)} %get-tuple-element.64, f32[8,512]{1,0:T(8,128)S(1)} %fusion.5, f32[8,512]{1,0:T(8,128)S(1)} %get-tuple-element.60, f32[4096,512,8]{1,0,2:T(8,128)} %get-tuple-element.61, pred[512,4096]{0,1:T(8,128)(4,1)S(1)} %fusion.8), kind=kLoop, calls=%fused_computation.13 | loop fusion | flops 134217728 | bytes 169918464 | tf_op jit(solution)/shard_map/reshape.17
  399.8 19.6 %convolution_bitcast_fusion.1 = f32[4096,1,256]{0,2,1:T(8,128)} fusion(bf16[8,512,4096]{1,2,0:T(8,128)(2,1)} %fusion.7, f32[512,8,256]{0,2,1:T(8,128)} %maximum_multiply_fusion, f32[512,8,256]{0,2,1:T(8,128)} %copy-done.5, f32[512,256]{0,1:T(8,128)} %get-tuple-element.55), kind=kOutput, calls=%fused_computation.36 | convolution fusion | flops 8593080320 | bytes 46661632 | tf_op jit(solution)/shard_map/kgqs,qkgd->skd/dot_general | solution.py:96
  419.5 44.2 %copy.123 = bf16[8,512,4096]{2,0,1:T(8,128)(2,1)} copy(bf16[8,512,4096]{1,2,0:T(8,128)(2,1)} %convert_bitcast_fusion) | data formatting | bytes 67108864 | tf_op jit(solution)/shard_map/reshape.9
  465.8 17.5 %convolution_bitcast_fusion = f32[4096,1,256]{0,2,1:T(8,128)} fusion(bf16[512,8,256]{2,1,0:T(8,128)(2,1)} %bitcast.205, bf16[8,512,4096]{2,0,1:T(8,128)(2,1)} %copy.123), kind=kOutput, calls=%fused_computation.35 | convolution fusion | flops 8589934592 | bytes 39845888 | tf_op jit(solution)/shard_map/kgqs,qkgd->skd/dot_general | solution.py:92
  484.3 16.1 %bitcast_multiply_fusion.1 = (f32[512,8,256]{0,2,1:T(8,128)S(1)}, bf16[256,8,512]{2,0,1:T(8,128)(2,1)S(1)}) fusion(f32[512,256]{0,1:T(8,128)S(1)} %copy-done.20, bf16[8,512,4096]{1,2,0:T(8,128)(2,1)} %fusion.7, bf16[4096,256]{0,1:T(8,128)(2,1)} %all-gather.10.cloned.1.call-done), kind=kOutput, calls=%fused_computation.56 | convolution fusion | flops 8593080320 | bytes 42467328 | tf_op jit(solution)/shard_map/kgqs,skd->qkgd/dot_general | solution.py:95
  507.6 6.1 fusion.105
  522.9 5.6 fusion.15
  531.8 13.6 %scatter_custom_fusion = bf16[2048,2048]{1,0:T(8,128)(2,1)} fusion(s32[512]{0:T(512)} %bitcast.211, bf16[]{:T(256)} %constant.44.clone.1, bf16[512,2048]{1,0:T(8,128)(2,1)} %get-tuple-element.36, pred[512]{0:T(512)(128)(4,1)S(1)} %copy-done.50), kind=kCustom, calls=%fused_computation.61 | custom fusion | flops 2097152 | bytes 10487296 | tf_op jit(solution)/shard_map/scatter-add | solution.py:152
  545.6 10.3 fusion.96
  555.9 8.4 fusion.90
  569.0 26.1 %reduce-scatter.8.cloned.1.call-done = bf16[256,2048]{1,0:T(8,128)(2,1)} async-done(((bf16[2048,2048]{1,0:T(8,128)(2,1)}), bf16[256,2048]{1,0:T(8,128)(2,1)}) %reduce-scatter.8.cloned.1.call-update) | async-done | bytes 1048592 | tf_op jit(solution)/shard_map/reduce_scatter | solution.py:153
  600.0 5.8 broadcast_in_dim.118
  605.8 15.6 %broadcast_in_dim.119 = bf16[1,4096,1152]{2,1,0:T(8,128)(2,1)} reshape(bf16[16,4,16,4,1152]{4,3,2,1,0:T(4,128)(2,1)} %broadcast_in_dim.118) | data formatting | bytes 18874368 | tf_op jit(solution)/shard_map/broadcast_in_dim | solution.py:61
  621.4 5.0 fusion.107
  626.4 476.3 %all-reduce.6 = (bf16[1152]{0:T(1024)(128)(2,1)}, bf16[1152,2048]{1,0:T(8,128)(2,1)}, bf16[2048]{0:T(1024)(128)(2,1)}, bf16[2048,2048]{1,0:T(8,128)(2,1)}, bf16[...) all-reduce(f32[1152]{0:T(1024)S(1)} %get-tuple-element.19, ...), channel_id=1, replica_groups=mesh['dp'=4,'cp'=8] {'cp'}, use_global_device_ids=true, to_apply=%region_22.23 | all-reduce | flops 11802240 | bytes 70813440 | tf_op jit(solution)/shard_map/psum | solution.py:158
  (224 shorter events, 79.1 us)
Async XLA Ops:
  7.2 152.3 %copy-start = (bf16[2048,256]{1,0:T(8,128)(2,1)S(1)}, bf16[2048,256]{1,0:T(8,128)(2,1)}, u32[]{:S(2)}) copy-start(bf16[2048,256]{1,0:T(8,128)(2,1)} %param.23) | copy-start | bytes 3145732
  7.2 84.0 %all-gather.6.cloned.1.call-start = ((), (), s32[]{:S(2)}) async-start(), calls=%async_computation.3 | async-start | bytes 9437184 | tf_op jit(solution)/shard_map/all_gather | solution.py:115
  25.2 11.8 %copy-start.60 = (bf16[1152]{0:T(1024)(128)(2,1)S(1)}, bf16[1152]{0:T(1024)(128)(2,1)}, u32[]{:S(2)}) copy-start(bf16[1152]{0:T(1024)(128)(2,1)} %param.18) | copy-start | bytes 6916
  43.2 128.6 %all-gather.10.cloned.1.call-start = ((), (), s32[]{:S(2)}) async-start(), calls=%async_computation.8 | async-start | bytes 2359296 | tf_op jit(solution)/shard_map/all_gather | solution.py:126
  44.1 56.8 %copy-start.49 = (pred[512]{0:T(512)(128)(4,1)}, pred[512]{0:T(512)(128)(4,1)S(1)}, u32[]{:S(2)}) copy-start(pred[512]{0:T(512)(128)(4,1)S(1)} %fusion.86) | copy-start | bytes 1540
  44.2 61.3 %copy-start.45 = (f32[256]{0:T(256)}, f32[256]{0:T(256)S(1)}, u32[]{:S(2)}) copy-start(f32[256]{0:T(256)S(1)} %convert_add_fusion.6) | copy-start | bytes 3076
  44.2 115.3 %copy-start.34 = (f32[2048]{0:T(1024)}, f32[2048]{0:T(1024)S(1)}, u32[]{:S(2)}) copy-start(f32[2048]{0:T(1024)S(1)} %convert_add_fusion.3) | copy-start | bytes 24580
  104.3 55.2 %copy-start.43 = (f32[512]{0:T(512)}, f32[512]{0:T(512)S(1)}, u32[]{:S(2)}) copy-start(f32[512]{0:T(512)S(1)} %fusion.87) | copy-start | bytes 6148
  105.4 12.0 %copy-start.36 = (f32[512]{0:T(512)}, f32[512]{0:T(512)S(1)}, u32[]{:S(2)}) copy-start(f32[512]{0:T(512)S(1)} %fusion.88) | copy-start | bytes 6148
  109.3 145.5 %all-gather.8.cloned.1.call-start = ((), (), s32[]{:S(2)}) async-start(), calls=%async_computation.7 | async-start | bytes 2359296 | tf_op jit(solution)/shard_map/all_gather | solution.py:127
  109.6 20.0 %copy-start.47 = (f32[256]{0:T(256)}, f32[256]{0:T(256)S(1)}, u32[]{:S(2)}) copy-start(f32[256]{0:T(256)S(1)} %convert_add_fusion.5) | copy-start | bytes 3076
  109.6 174.2 %copy-start.39 = (f32[2048]{0:T(1024)}, f32[2048]{0:T(1024)S(1)}, u32[]{:S(2)}) copy-start(f32[2048]{0:T(1024)S(1)} %convert_add_fusion.2) | copy-start | bytes 24580
  129.6 21.9 %copy-start.28 = (f32[512,8]{0,1:T(8,128)}, f32[512,8]{0,1:T(8,128)S(1)}, u32[]{:S(2)}) copy-start(f32[512,8]{0,1:T(8,128)S(1)} %fusion.85) | copy-start | bytes 49156
  162.6 351.1 %reduce-scatter.4.cloned.1.call-start = ((), (), s32[]{:S(2)}) async-start(), calls=%async_computation.4 | async-start | bytes 4718592 | tf_op jit(solution)/shard_map/reduce_scatter | solution.py:137
  270.5 9.3 copy-start.3
  270.5 9.3 copy-start.9
  283.9 9.7 copy-start.64
  419.4 44.3 %copy-start.18 = (bf16[512,2048]{1,0:T(8,128)(2,1)S(1)}, bf16[512,2048]{1,0:T(8,128)(2,1)}, u32[]{:S(2)}) copy-start(bf16[512,2048]{1,0:T(8,128)(2,1)} %convolution_convert_fusion) | copy-start | bytes 6291460
  419.4 103.5 %reduce-scatter.6.cloned.1.call-start = ((), (), s32[]{:S(2)}) async-start(), calls=%async_computation.5 | async-start | bytes 4718592 | tf_op jit(solution)/shard_map/reduce_scatter | solution.py:138
  483.3 111.7 %reduce-scatter.8.cloned.1.call-start = ((), (), s32[]{:S(2)}) async-start(), calls=%async_computation.6 | async-start | bytes 9437184 | tf_op jit(solution)/shard_map/reduce_scatter | solution.py:153
  545.5 10.3 copy-start.11
  545.5 10.3 copy-start.22
  545.5 10.3 copy-start.40
  545.6 10.3 copy-start.59
  545.6 10.3 copy-start.65
  545.6 10.3 copy-start.69
  566.6 28.4 %copy-start.33 = (f32[1152]{0:T(1024)S(1)}, f32[1152]{0:T(1024)}, u32[]{:S(2)}) copy-start(f32[1152]{0:T(1024)} %copy-done.32) | copy-start | bytes 13828
  566.6 28.4 %copy-start.54 = (f32[256]{0:T(256)S(1)}, f32[256]{0:T(256)}, u32[]{:S(2)}) copy-start(f32[256]{0:T(256)} %copy-done.53) | copy-start | bytes 3076
  569.0 30.6 %copy-start.52 = (f32[256]{0:T(256)S(1)}, f32[256]{0:T(256)}, u32[]{:S(2)}) copy-start(f32[256]{0:T(256)} %copy-done.51) | copy-start | bytes 3076
  569.0 30.6 %copy-start.14 = (bf16[16,16,1152]{2,1,0:T(8,128)(2,1)S(1)}, bf16[16,16,1152]{2,1,0:T(8,128)(2,1)}, u32[]{:S(2)}) copy-start(bf16[16,16,1152]{2,1,0:T(8,128)(2,1)} %copy-done.13) | copy-start | bytes 1769476
  605.8 15.6 %copy-start.16 = (bf16[256,1152]{1,0:T(8,128)(2,1)S(1)}, bf16[256,1152]{1,0:T(8,128)(2,1)}, u32[]{:S(2)}) copy-start(bf16[256,1152]{1,0:T(8,128)(2,1)} %copy-done.15) | copy-start | bytes 1769476
  605.8 15.6 %copy-start.24 = (bf16[256,2048]{1,0:T(8,128)(2,1)S(1)}, bf16[256,2048]{1,0:T(8,128)(2,1)}, u32[]{:S(2)}) copy-start(bf16[256,2048]{1,0:T(8,128)(2,1)} %reduce-scatter.8.cloned.1.call-done) | copy-start | bytes 3145732
  (46 other events, 195.7 us)
Sparse Core Ops, SparseCore 0:
  43.3 47.8 all-gather.5
  109.4 22.9 all-gather.9
  162.7 22.9 all-gather.7
  419.5 34.9 reduce-scatter.3
  483.4 34.9 reduce-scatter.5
  545.6 49.3 reduce-scatter.7
where the time goes:
time: 1120 us; the launch traced here: 1110 us
  blocking collectives  476 us (42%)
  matrix products  232 us (21%)
  other arithmetic  180 us (16%)
  local copies, waits for them, and re-layouts  135 us (12%)
  waiting for transfers between devices  70.2 us (6%)
  between operations  15.6 us (1%)
    psum x1, blocking collectives, device_body(): lax.psum((g_pn, g_proj, g_pre, g_query, g_key, g_value, g_q_gain, g_k_gai...  476 us
    another operation x2, other arithmetic  87.2 us
    dot_general x1, matrix products, attn_backward(): jnp.einsum('qkgd,skd->kgqs', d_grp, v_all, preferred_element_type=jnp.flo...  52.7 us
    another operation x1, local copies, waits for them, and re-layouts  44.2 us
    all_gather x1, waiting for transfers between devices, device_body(): soft_all = lax.all_gather(soft_loc, 'cp', tiled=True)  43.9 us
    dot_general x1, matrix products, attn_forward(): jnp.einsum('qkgd,skd->kgqs', q_grp, k_all, preferred_element_type=jnp.flo...  27.7 us
    reduce_scatter x1, waiting for transfers between devices, device_body(): lax.psum_scatter(d_soft_all, 'cp', scatter_dimension=0, tiled=True)  26.1 us
  transfers between devices with their start and end apart: 6, of which 2 were waited for; matrix products, arithmetic and copies ran while one was open for 24% of the time, Pallas kernels for 0%

commit v1 on v0

v1 whole, which is shorter than its diff:
```python
import functools
import jax
import jax.numpy as jnp
from jax import lax
from jax.experimental import pallas as pl
from jax.experimental.pallas import tpu as pltpu
from jax.sharding import PartitionSpec as P

GRID = 64
POOL = 4
EPS = 1e-6
ROPE_BASE = 1000000.0
ROPE_SCALE = 8.0
NEG_BIG = -1e30
STRIPS = 4
ROWS = 256
F32 = jnp.float32
BF16 = jnp.bfloat16
ONE_BUF = pl.Buffered(1)


def dot_nn(lhs, rhs):
    return lax.dot_general(lhs, rhs, (((1,), (0,)), ((), ())), preferred_element_type=F32)


def dot_nt(lhs, rhs):
    return lax.dot_general(lhs, rhs, (((1,), (1,)), ((), ())), preferred_element_type=F32)


def inv_rms(wide):
    return lax.rsqrt(jnp.mean(wide * wide, axis=-1, keepdims=True) + EPS)


def norm_back(d_out, wide, inv, gain1):
    d_scaled = d_out * gain1
    unit = wide * inv
    d_in = inv * (d_scaled - unit * jnp.mean(d_scaled * unit, axis=-1, keepdims=True))
    d_gain = jnp.sum(d_out * unit, axis=0, keepdims=True)
    return d_in, d_gain


def resident(shape, col=None):
    if col is None:
        return pl.BlockSpec(shape, lambda *_: (0,) * len(shape), pipeline_mode=ONE_BUF)
    return pl.BlockSpec(shape, lambda *_: (0, col), pipeline_mode=ONE_BUF)


def pool_matrix(out_rows, in_rows, transpose):
    side = GRID // POOL
    shape = (in_rows, out_rows) if transpose else (out_rows, in_rows)
    out_id = lax.broadcasted_iota(jnp.int32, shape, 1 if transpose else 0)
    in_id = lax.broadcasted_iota(jnp.int32, shape, 0 if transpose else 1)
    target = (in_id // (GRID * POOL)) * side + (in_id % GRID) // POOL
    return jnp.where(out_id == target, 1.0, 0.0).astype(BF16)


def pool_kernel(vis_ref, gain_ref, pooled_ref, normed_ref):
    weights = pool_matrix(pooled_ref.shape[0], vis_ref.shape[0], False)
    pooled = (dot_nn(weights, vis_ref[...]) * (1.0 / (POOL * POOL))).astype(BF16)
    pooled_ref[...] = pooled
    wide = pooled.astype(F32)
    normed_ref[...] = (wide * inv_rms(wide) * (1.0 + gain_ref[...])).astype(BF16)


def pool_and_norm(vis_rows, gain):
    rows, dim = vis_rows.shape
    step_in = STRIPS * GRID * POOL
    step_out = step_in // (POOL * POOL)
    out = jax.ShapeDtypeStruct((rows // (POOL * POOL), dim), BF16)
    out_spec = pl.BlockSpec((step_out, dim), lambda i: (i, 0))
    return pl.pallas_call(
        pool_kernel, grid=(rows // step_in,),
        in_specs=[pl.BlockSpec((step_in, dim), lambda i: (i, 0)), resident((1, dim))],
        out_specs=[out_spec, out_spec], out_shape=[out, out],
        cost_estimate=pl.CostEstimate(flops=2 * rows * dim * step_out, bytes_accessed=rows * dim * 2, transcendentals=0),
        name='pool')(vis_rows, gain)


def unpool_kernel(d_ref, pooled_ref, gain_ref, out_ref, g_ref):
    wide = pooled_ref[...].astype(F32)
    d_pooled, d_gain = norm_back(d_ref[...].astype(F32), wide, inv_rms(wide), 1.0 + gain_ref[...])

    @pl.when(pl.program_id(0) == 0)
    def _():
        g_ref[...] = jnp.zeros_like(g_ref)

    g_ref[...] += d_gain
    spread = (d_pooled.astype(BF16).astype(F32) * (1.0 / (POOL * POOL))).astype(BF16)
    out_ref[...] = dot_nn(pool_matrix(spread.shape[0], out_ref.shape[0], True), spread).astype(BF16)


def unpool(d_normed, pooled, gain):
    rows, dim = pooled.shape
    step_out = STRIPS * GRID * POOL
    step_in = step_out // (POOL * POOL)
    in_spec = pl.BlockSpec((step_in, dim), lambda i: (i, 0))
    return pl.pallas_call(
        unpool_kernel, grid=(rows // step_in,),
        in_specs=[in_spec, in_spec, resident((1, dim))],
        out_specs=[pl.BlockSpec((step_out, dim), lambda i: (i, 0)), pl.BlockSpec((1, dim), lambda i: (0, 0))],
        out_shape=[jax.ShapeDtypeStruct((rows * POOL * POOL, dim), BF16), jax.ShapeDtypeStruct((1, dim), F32)],
        cost_estimate=pl.CostEstimate(flops=32 * rows * dim * step_in, bytes_accessed=32 * rows * dim, transcendentals=0),
        name='unpool')(d_normed, pooled, gain)


def rotate(unit, cos, sin):
    half = cos.shape[-1]
    first, second = unit[:, :half], unit[:, half:]
    return jnp.concatenate([first * cos - second * sin, second * cos + first * sin], axis=-1)


def rotate_back(d_out, cos, sin):
    half = cos.shape[-1]
    first, second = d_out[:, :half], d_out[:, half:]
    return jnp.concatenate([first * cos + second * sin, second * cos - first * sin], axis=-1)


def front_kernel(row_ref, text_ref, all_ref, wp_ref, pre_ref, wk_ref, wv_ref, kg_ref, cos_ref, sin_ref,
                 rows_ref, merged_ref, hidden_ref, kraw_ref, kv_ref):
    row_id = row_ref[...]
    cols = lax.broadcasted_iota(jnp.int32, (row_id.shape[0], all_ref.shape[0]), 1)
    pick = jnp.where(cols == row_id, 1.0, 0.0).astype(BF16)
    normed_rows = dot_nn(pick, all_ref[...]).astype(BF16)
    rows_ref[...] = normed_rows
    soft = dot_nn(normed_rows, wp_ref[...]).astype(BF16)
    wide = jnp.where(row_id >= 0, soft.astype(F32), text_ref[...].astype(F32))
    merged_ref[...] = wide.astype(BF16)
    hidden = (wide * inv_rms(wide) * (1.0 + pre_ref[...])).astype(BF16)
    hidden_ref[...] = hidden
    k_raw = dot_nn(hidden, wk_ref[...]).astype(BF16)
    kraw_ref[...] = k_raw
    k_wide = k_raw.astype(F32)
    unit = k_wide * inv_rms(k_wide) * (1.0 + kg_ref[...])
    head = k_raw.shape[1]
    kv_ref[:, :head] = rotate(unit, cos_ref[...], sin_ref[...]).astype(BF16)
    kv_ref[:, head:] = dot_nn(hidden, wv_ref[...]).astype(BF16)


def front(row_id, text, normed_all, w_proj, pre_gain, w_key, w_value, k_gain, cos, sin):
    seq, dim = text.shape
    n_img, dim_v = normed_all.shape
    head = w_key.shape[1]

    def by_row(width):
        return pl.BlockSpec((ROWS, width), lambda i: (i, 0))

    flops = 2 * seq * (n_img * dim_v + dim_v * dim + 2 * dim * head)
    return pl.pallas_call(
        front_kernel, grid=(seq // ROWS,),
        in_specs=[by_row(1), by_row(dim), resident(normed_all.shape), resident(w_proj.shape), resident((1, dim)),
                  resident(w_key.shape), resident(w_value.shape), resident((1, head)), by_row(cos.shape[1]), by_row(cos.shape[1])],
        out_specs=[by_row(dim_v), by_row(dim), by_row(dim), by_row(head), by_row(2 * head)],
        out_shape=[jax.ShapeDtypeStruct((seq, w), BF16) for w in (dim_v, dim, dim, head, 2 * head)],
        cost_estimate=pl.CostEstimate(flops=flops, bytes_accessed=flops // 200, transcendentals=0),
        name='front')(row_id, text, normed_all, w_proj, pre_gain, w_key, w_value, k_gain, cos, sin)


def query_kernel(hid_ref, wq_ref, qg_ref, cos_ref, sin_ref, qraw_ref, qs_ref):
    q_raw = dot_nn(hid_ref[...], wq_ref[...]).astype(BF16)
    qraw_ref[...] = q_raw
    wide = q_raw.astype(F32)
    unit = wide * inv_rms(wide) * (1.0 + qg_ref[...])
    q_head = rotate(unit, cos_ref[...], sin_ref[...]).astype(BF16)
    qs_ref[...] = (q_head.astype(F32) * q_head.shape[1] ** -0.5).astype(BF16)


def query(hidden, w_query, q_gain, cos, sin):
    seq, dim = hidden.shape
    head = q_gain.shape[1]
    heads = w_query.shape[1] // head
    out = jax.ShapeDtypeStruct((seq, heads * head), BF16)
    by_head = pl.BlockSpec((seq, head), lambda h: (0, h))
    return pl.pallas_call(
        query_kernel, grid=(heads,),
        in_specs=[resident(hidden.shape), pl.BlockSpec((dim, head), lambda h: (0, h)), resident((1, head)),
                  resident(cos.shape), resident(sin.shape)],
        out_specs=[by_head, by_head], out_shape=[out, out],
        cost_estimate=pl.CostEstimate(flops=2 * seq * dim * heads * head, bytes_accessed=dim * heads * head * 2, transcendentals=0),
        name='query')(hidden, w_query, q_gain, cos, sin)


def visible_mask(key_base, q_base, start, shape, block_len):
    key_pos = key_base + lax.broadcasted_iota(jnp.int32, shape, 0)
    q_pos = q_base + lax.broadcasted_iota(jnp.int32, shape, 1)
    return (key_pos <= q_pos) | ((key_pos >= start) & (key_pos < start + block_len))


def key_rows(index, width):
    return pl.ds(pl.multiple_of(index * width, width), width)


def attn_kernel(block_len, pair, rank_ref, qs_ref, k_ref, v_ref, start_ref, o_ref, lse_ref, vt_ref, acc_ref, m_ref, l_ref):
    seq = qs_ref.shape[0]
    head = k_ref.shape[1]
    total = k_ref.shape[0]
    rank = rank_ref[0]
    start = start_ref[...]

    @pl.when(pl.program_id(0) == 0)
    def _():
        @pl.loop(0, total // seq)
        def _(i):
            vt_ref[:, key_rows(i, seq)] = v_ref[key_rows(i, seq), :].astype(F32).T.astype(BF16)

    def block(base, width, masked, first):
        rows = pl.ds(pl.multiple_of(base, width), width)
        k_blk = k_ref[rows, :]
        vt_blk = vt_ref[:, rows]
        if masked:
            mask = visible_mask(base, rank * seq, start, (width, seq), block_len)
        scores = [dot_nt(k_blk, qs_ref[:, j * head:(j + 1) * head]) for j in range(pair)]
        for j in range(pair):
            score = jnp.where(mask, scores[j], NEG_BIG) if masked else scores[j]
            top = jnp.max(score, axis=0, keepdims=True)
            if first:
                m_new = top
                prob = jnp.exp(score - m_new)
                l_ref[j] = jnp.sum(prob, axis=0, keepdims=True)
                acc_ref[j] = dot_nn(vt_blk, prob.astype(BF16))
            else:
                m_old = m_ref[j]
                m_new = jnp.maximum(m_old, top)
                alpha = jnp.exp(m_old - m_new)
                prob = jnp.exp(score - m_new)
                l_ref[j] = l_ref[j] * alpha + jnp.sum(prob, axis=0, keepdims=True)
                acc_ref[j] = acc_ref[j] * alpha + dot_nn(vt_blk, prob.astype(BF16))
            m_ref[j] = m_new

    block(rank * seq, seq, True, True)

    @pl.when(rank * seq + seq < total)
    def _():
        block((rank + 1) * seq, block_len, True, False)

    @pl.loop(0, rank)
    def _(i):
        block(i * seq, seq, False, False)

    for j in range(pair):
        denom = l_ref[j]
        o_ref[:, j * head:(j + 1) * head] = (acc_ref[j] / denom).T.astype(BF16)
        lse_ref[j] = m_ref[j] + jnp.log(denom)


def attention(rank, qs, kv_all, blk_start, head, block_len):
    seq, width = qs.shape
    heads = width // head
    pair = 2 if heads % 2 == 0 else 1
    total = kv_all.shape[0]
    flops = 4 * seq * heads * head * total
    by_head = pl.BlockSpec((seq, pair * head), lambda h, *_: (0, h))
    grid_spec = pltpu.PrefetchScalarGridSpec(
        num_scalar_prefetch=1, grid=(heads // pair,),
        in_specs=[by_head, resident((total, head), 0), resident((total, head), 1), resident((1, seq))],
        out_specs=[by_head, pl.BlockSpec((pair, 1, seq), lambda h, *_: (h, 0, 0))],
        scratch_shapes=[pltpu.VMEM((head, total), BF16), pltpu.VMEM((pair, head, seq), F32),
                        pltpu.VMEM((pair, 1, seq), F32), pltpu.VMEM((pair, 1, seq), F32)])
    return pl.pallas_call(
        functools.partial(attn_kernel, block_len, pair), grid_spec=grid_spec,
        out_shape=[jax.ShapeDtypeStruct((seq, width), BF16), jax.ShapeDtypeStruct((heads, 1, seq), F32)],
        cost_estimate=pl.CostEstimate(flops=flops, bytes_accessed=flops // 1000, transcendentals=0),
        name='attention')(rank, qs, kv_all, kv_all, blk_start)


def post_kernel(o_ref, merged_ref, dy_ref, wo_ref, gain_ref, y_ref, dproj_ref, dattn_ref, g_ref):
    proj = dot_nn(o_ref[...], wo_ref[...]).astype(BF16).astype(F32)
    inv = inv_rms(proj)
    gain1 = 1.0 + gain_ref[...]
    y_ref[...] = (merged_ref[...].astype(F32) + proj * inv * gain1).astype(BF16)
    d_in, d_gain = norm_back(dy_ref[...].astype(F32), proj, inv, gain1)

    @pl.when(pl.program_id(0) == 0)
    def _():
        g_ref[...] = jnp.zeros_like(g_ref)

    g_ref[...] += d_gain
    d_proj = d_in.astype(BF16)
    dproj_ref[...] = d_proj
    dattn_ref[...] = dot_nt(d_proj, wo_ref[...]).astype(BF16)


def post(attn_out, merged, grad_y, w_out, gain):
    seq, dim = merged.shape
    width = attn_out.shape[1]

    def by_row(cols):
        return pl.BlockSpec((ROWS, cols), lambda i: (i, 0))

    flops = 4 * seq * dim * width
    return pl.pallas_call(
        post_kernel, grid=(seq // ROWS,),
        in_specs=[by_row(width), by_row(dim), by_row(dim), resident(w_out.shape), resident((1, dim))],
        out_specs=[by_row(dim), by_row(dim), by_row(width), pl.BlockSpec((1, dim), lambda i: (0, 0))],
        out_shape=[jax.ShapeDtypeStruct((seq, dim), BF16), jax.ShapeDtypeStruct((seq, dim), BF16),
                   jax.ShapeDtypeStruct((seq, width), BF16), jax.ShapeDtypeStruct((1, dim), F32)],
        cost_estimate=pl.CostEstimate(flops=flops, bytes_accessed=flops // 200, transcendentals=0),
        name='post')(attn_out, merged, grad_y, w_out, gain)


def back_kernel(block_len, pair, rank_ref, qs_ref, do_ref, o_ref, k_ref, v_ref, start_ref, lse_ref, qraw_ref, cos_ref, sin_ref, gain_ref,
                dq_ref, g_ref, dkv_ref, kt_ref, acc_ref):
    seq = qs_ref.shape[0]
    head = k_ref.shape[1]
    total = k_ref.shape[0]
    rank = rank_ref[0]
    start = start_ref[...]

    @pl.when(pl.program_id(0) == 0)
    def _():
        g_ref[...] = jnp.zeros_like(g_ref)

        @pl.loop(0, total // seq)
        def _(i):
            kt_ref[:, key_rows(i, seq)] = k_ref[key_rows(i, seq), :].astype(F32).T.astype(BF16)
            dkv_ref[key_rows(i, seq), :] = jnp.zeros((seq, 2 * head), F32)

    cols = [slice(j * head, (j + 1) * head) for j in range(pair)]
    deltas = []
    for j in range(pair):
        both = do_ref[:, cols[j]].astype(F32) * o_ref[:, cols[j]].astype(F32)
        delta = jnp.sum(both, axis=1, keepdims=True)
        deltas.append(jnp.broadcast_to(delta, (seq, 128)).T[0:1, :])
    acc_ref[...] = jnp.zeros_like(acc_ref)

    def block(base, width, masked):
        rows = pl.ds(pl.multiple_of(base, width), width)
        k_blk = k_ref[rows, :]
        v_blk = v_ref[rows, :]
        kt_blk = kt_ref[:, rows]
        if masked:
            mask = visible_mask(base, rank * seq, start, (width, seq), block_len)
        d_k = None
        d_v = None
        for j in range(pair):
            qs = qs_ref[:, cols[j]]
            d_o = do_ref[:, cols[j]]
            score = dot_nt(k_blk, qs)
            if masked:
                score = jnp.where(mask, score, NEG_BIG)
            prob = jnp.exp(score - lse_ref[j])
            d_score = (prob * (dot_nt(v_blk, d_o) - deltas[j])).astype(BF16)
            v_part = dot_nn(prob.astype(BF16), d_o)
            k_part = dot_nn(d_score, qs)
            d_v = v_part if d_v is None else d_v + v_part
            d_k = k_part if d_k is None else d_k + k_part
            acc_ref[j] += dot_nn(kt_blk, d_score)
        dkv_ref[rows, :head] += d_k
        dkv_ref[rows, head:] += d_v

    block(rank * seq, seq, True)

    @pl.when(rank * seq + seq < total)
    def _():
        block((rank + 1) * seq, block_len, True)

    @pl.loop(0, rank)
    def _(i):
        block(i * seq, seq, False)

    gain1 = 1.0 + gain_ref[...]
    for j in range(pair):
        d_q = (acc_ref[j] * head ** -0.5).T.astype(BF16).astype(F32)
        d_unit = rotate_back(d_q, cos_ref[...], sin_ref[...])
        wide = qraw_ref[:, cols[j]].astype(F32)
        d_raw, d_gain = norm_back(d_unit, wide, inv_rms(wide), gain1)
        dq_ref[:, cols[j]] = d_raw.astype(BF16)
        g_ref[...] += d_gain


def attention_back(rank, qs, d_attn, attn_out, kv_all, blk_start, lse, q_raw, cos, sin, q_gain, block_len):
    seq, width = qs.shape
    head = q_gain.shape[1]
    heads = width // head
    pair = 2 if heads % 2 == 0 else 1
    total = kv_all.shape[0]
    flops = 10 * seq * heads * head * total
    by_head = pl.BlockSpec((seq, pair * head), lambda h, *_: (0, h))
    grid_spec = pltpu.PrefetchScalarGridSpec(
        num_scalar_prefetch=1, grid=(heads // pair,),
        in_specs=[by_head, by_head, by_head, resident((total, head), 0), resident((total, head), 1), resident((1, seq)),
                  pl.BlockSpec((pair, 1, seq), lambda h, *_: (h, 0, 0)), by_head, resident(cos.shape), resident(sin.shape), resident((1, head))],
        out_specs=[by_head, pl.BlockSpec((1, head), lambda h, *_: (0, 0)), resident((total, 2 * head))],
        scratch_shapes=[pltpu.VMEM((head, total), BF16), pltpu.VMEM((pair, head, seq), F32)])
    return pl.pallas_call(
        functools.partial(back_kernel, block_len, pair), grid_spec=grid_spec,
        out_shape=[jax.ShapeDtypeStruct((seq, width), BF16), jax.ShapeDtypeStruct((1, head), F32),
                   jax.ShapeDtypeStruct((total, 2 * head), F32)],
        cost_estimate=pl.CostEstimate(flops=flops, bytes_accessed=flops // 1000, transcendentals=0),
        name='attention_back')(rank, qs, d_attn, attn_out, kv_all, kv_all, blk_start, lse, q_raw, cos, sin, q_gain)


def merge_layout(img_pos, dev_rank, seq_loc, block_len):
    q_pos = dev_rank * seq_loc + jnp.arange(seq_loc)
    offset = q_pos[:, None] - img_pos[None, :]
    in_blk = (offset >= 0) & (offset < block_len)
    is_img = jnp.any(in_blk, axis=1)
    flat_row = jnp.sum(jnp.where(in_blk, jnp.arange(img_pos.shape[0])[None, :] * block_len + offset, 0), axis=1)
    blk_start = jnp.where(is_img, q_pos - jnp.sum(jnp.where(in_blk, offset, 0), axis=1), -block_len)
    return q_pos, is_img, jnp.where(is_img, flat_row, -1), blk_start


def rope_tables(positions, head_dim):
    inv_freq = ROPE_BASE ** (-jnp.arange(0, head_dim, 2).astype(F32) / head_dim)
    angle = (positions.astype(F32) / ROPE_SCALE)[:, None] * inv_freq[None, :]
    return jnp.cos(angle), jnp.sin(angle)


def scatter_sum(partial):
    return lax.psum_scatter(partial, 'cp', scatter_dimension=0, tiled=True)


def solution(mesh):
    seq_spec = P(('dp', 'cp'))
    part_spec = P('dp')
    rep_spec = P()

    def device_body(vis_loc, text_loc, img_pos, grad_y, pn_gain, w_proj, pre_gain, w_query, w_key, w_value, q_gain, k_gain, w_out, post_gain):
        rank = lax.axis_index('cp')
        seq = text_loc.shape[0]
        dim_v = vis_loc.shape[2]
        head = q_gain.shape[0]
        block_len = (GRID // POOL) ** 2
        pn_row, pre_row, q_row, k_row, post_row = (g.astype(F32)[None, :] for g in (pn_gain, pre_gain, q_gain, k_gain, post_gain))
        q_pos, is_img, flat_row, blk_start = merge_layout(img_pos, rank, seq, block_len)
        cos, sin = rope_tables(q_pos, head)
        rank_arr = rank.astype(jnp.int32)[None]
        start_row = blk_start.astype(jnp.int32)[None, :]
        img_mask = is_img[:, None]

        pooled, normed = pool_and_norm(vis_loc.reshape(-1, dim_v), pn_row)
        normed_all = lax.all_gather(normed, 'cp', tiled=True)
        normed_rows, merged, hidden, k_raw, kv_loc = front(
            flat_row.astype(jnp.int32)[:, None], text_loc, normed_all, w_proj, pre_row, w_key, w_value, k_row, cos, sin)
        kv_all = lax.all_gather(kv_loc, 'cp', tiled=True)
        q_raw, qs = query(hidden, w_query, q_row, cos, sin)
        attn_out, lse = attention(rank_arr, qs, kv_all, start_row, head, block_len)
        y_loc, d_proj, d_attn, g_post = post(attn_out, merged, grad_y, w_out, post_row)
        g_out = scatter_sum(jnp.einsum('sh,sd->hd', attn_out, d_proj, preferred_element_type=F32))
        d_q, g_q_gain, dkv_part = attention_back(
            rank_arr, qs, d_attn, attn_out, kv_all, start_row, lse, q_raw, cos, sin, q_row, block_len)
        dkv = scatter_sum(dkv_part)
        g_query = scatter_sum(jnp.einsum('sd,sh->dh', hidden, d_q, preferred_element_type=F32))

        d_k = dkv[:, :head].astype(BF16).astype(F32)
        d_v = dkv[:, head:].astype(BF16)
        k_wide = k_raw.astype(F32)
        d_k_raw, g_k_gain = norm_back(rotate_back(d_k, cos, sin), k_wide, inv_rms(k_wide), 1.0 + k_row)
        d_kv = jnp.concatenate([d_k_raw.astype(BF16), d_v], axis=1)
        w_kv = jnp.concatenate([w_key, w_value], axis=1)
        d_hidden = jnp.einsum('sh,dh->sd', d_q, w_query, preferred_element_type=F32)
        d_hidden = (d_hidden + jnp.einsum('sh,dh->sd', d_kv, w_kv, preferred_element_type=F32)).astype(BF16)
        m_wide = merged.astype(F32)
        d_norm, g_pre = norm_back(d_hidden.astype(F32), m_wide, inv_rms(m_wide), 1.0 + pre_row)
        d_merged = (grad_y.astype(F32) + d_norm.astype(BF16).astype(F32)).astype(BF16)
        grad_text = jnp.where(img_mask, 0.0, d_merged).astype(BF16)
        d_soft = jnp.where(img_mask, d_merged, 0.0).astype(BF16)
        d_normed_rows = jnp.einsum('nd,cd->nc', d_soft, w_proj, preferred_element_type=F32).astype(BF16)
        pick = (flat_row[:, None] == jnp.arange(normed_all.shape[0])[None, :]).astype(BF16)
        d_normed_all = jnp.einsum('sn,sc->nc', pick, d_normed_rows, preferred_element_type=F32).astype(BF16)
        d_normed = scatter_sum(d_normed_all)
        g_kv = jnp.einsum('sd,sh->dh', hidden, d_kv, preferred_element_type=F32)
        g_proj_t = jnp.einsum('nd,nc->dc', d_soft, normed_rows, preferred_element_type=F32)
        g_mix = scatter_sum(jnp.concatenate([g_kv, g_proj_t], axis=1))
        grad_vis, g_pn = unpool(d_normed, pooled, pn_row)

        small = [g_pn[0], g_pre[0], g_q_gain[0], g_k_gain[0], g_post[0]]
        small_sum = lax.psum(jnp.concatenate(small), 'cp').astype(BF16)
        cuts = [0]
        for part in small:
            cuts.append(cuts[-1] + part.shape[0])
        g_pn, g_pre, g_q_gain, g_k_gain, g_post = (small_sum[a:b] for a, b in zip(cuts[:-1], cuts[1:]))
        g_mix = lax.all_gather(g_mix.astype(BF16), 'cp', tiled=True)
        g_out = lax.all_gather(g_out.astype(BF16), 'cp', tiled=True)
        g_query = lax.all_gather(g_query.astype(BF16), 'cp', tiled=True)
        g_key, g_value, g_proj = g_mix[:, :head], g_mix[:, head:2 * head], g_mix[:, 2 * head:].T
        return (y_loc, grad_text, grad_vis.reshape(vis_loc.shape), g_pn, g_proj, g_pre, g_query, g_key, g_value, g_q_gain, g_k_gain, g_out, g_post)

    in_specs = (seq_spec, seq_spec, part_spec, seq_spec) + (rep_spec,) * 10
    out_specs = (seq_spec, seq_spec, seq_spec) + (part_spec,) * 10
    return jax.shard_map(device_body, mesh=mesh, in_specs=in_specs, out_specs=out_specs, check_vma=False)
```

time: 1120 us -> 745 us (0.67)
  blocking collectives: 476 us -> 25.2 us
  waiting for transfers between devices: 70.2 us -> 409 us
  matrix products: 232 us -> 52.6 us
  Pallas kernels: 0 us -> 165 us
  other arithmetic: 180 us -> 32.5 us
  local copies, waits for them, and re-layouts: 135 us -> 37 us
    psum x1, blocking collectives: 476 us -> 25.2 us  [device_body(): small_sum = lax.psum(jnp.concatenate(small), 'cp').astype(BF16)]
    reduce_scatter x3 -> x5, waiting for transfers between devices: 26.1 us -> 257 us  [scatter_sum(): return lax.psum_scatter(partial, 'cp', scatter_dimension=0, tiled=True)]
    dot_general x21 -> x7, matrix products: 232 us -> 52.6 us  [the longest x1 10.6 us: device_body(): d_hidden = jnp.einsum('sh,dh->sd', d_q, w_query, preferred_element_type=F32)]
    pallas_call x0 -> x7, Pallas kernels: none -> 165 us  [the longest x1 66.5 us: attention_back(): pl.pallas_call(functools.partial(back_kernel, block_len, pair), grid_spec...]
    all_gather x3 -> x5, waiting for transfers between devices: 43.9 us -> 152 us  [the longest x1 48.8 us: device_body(): g_out = lax.all_gather(g_out.astype(BF16), 'cp', tiled=True)]
    another operation x2 -> x1, other arithmetic: 87.2 us -> 1.38 us
    reduce_sum x8 -> x3, other arithmetic: 48.5 us -> 0.9 us  [the longest x2 0.63 us: inv_rms(): return lax.rsqrt(jnp.mean(wide * wide, axis=-1, keepdims=True) + EPS)]
    another operation x1 -> x0, local copies, waits for them, and re-layouts: 44.2 us -> none
  transfers between devices with their start and end apart: 6 -> 10, of which waited for: 2 -> 10; matrix products, arithmetic and copies ran while one was open for 24% -> 12% of each run, Pallas kernels for 0% -> 3%
where the time goes in v1:
time: 745 us; the launch traced here: 738 us
  waiting for transfers between devices  409 us (55%)
  Pallas kernels  165 us (22%)
  matrix products  52.6 us (7%)
  local copies, waits for them, and re-layouts  37 us (5%)
  other arithmetic  32.5 us (4%)
  blocking collectives  25.2 us (3%)
  between operations  14.7 us (2%)
    reduce_scatter x5, waiting for transfers between devices, scatter_sum(): return lax.psum_scatter(partial, 'cp', scatter_dimension=0, tiled=True)  257 us
    pallas_call x1, Pallas kernels, attention_back(): pl.pallas_call(functools.partial(back_kernel, block_len, pair), grid_spec...  66.5 us
    all_gather x1, waiting for transfers between devices, device_body(): g_out = lax.all_gather(g_out.astype(BF16), 'cp', tiled=True)  48.8 us
    all_gather x1, waiting for transfers between devices, device_body(): g_mix = lax.all_gather(g_mix.astype(BF16), 'cp', tiled=True)  46.4 us
    pallas_call x1, Pallas kernels, attention(): pl.pallas_call(functools.partial(attn_kernel, block_len, pair), grid_spec...  42.2 us
    all_gather x1, waiting for transfers between devices, device_body(): normed_all = lax.all_gather(normed, 'cp', tiled=True)  28.2 us
    unnamed x44, local copies, waits for them, and re-layouts  26.2 us
    psum x1, blocking collectives, device_body(): small_sum = lax.psum(jnp.concatenate(small), 'cp').astype(BF16)  25.2 us
  transfers between devices with their start and end apart: 10, of which 10 were waited for; matrix products, arithmetic and copies ran while one was open for 12% of the time, Pallas kernels for 3%

profile of v1, /device:TPU:87, one launch (start us, length us, event | category | flops | bytes accessed | tf_op | source)
XLA Modules:
  0.0 738.3 jit_solution(15595559420452323658)
XLA Ops:
  8.5 6.3 pool.1
  19.1 28.2 %all-gather.6.cloned.1.call-done.all_ref = bf16[2048,1152]{1,0:T(8,128)(2,1)} async-done(((bf16[256,1152]{1,0:T(8,128)(2,1)}), bf16[2048,1152]{1,0:T(8,128)(2,1)}) %all-gather.6.cloned.1.call-update) | async-done | bytes 4718608 | tf_op jit(solution)/shard_map/all_gather | solution.py:431
  47.3 14.0 %front.1 = (bf16[512,1152]{1,0:T(8,128)(2,1)}, bf16[512,2048]{1,0:T(8,128)(2,1)}, bf16[512,2048]{1,0:T(8,128)(2,1)}, bf16[512,256]{1,0:T(8,128)(2,1)}, bf16[512,512]{1,0:T(8,128)(2,1)}) custom-call(s32[512,1]{1,0:T(8,128)} %copy.32.row_ref, bf16[512,2048]{1,0:T(8,128)(2,1)} %text_ref.1, bf16[2048,1152]{1,0:T(8,128)(2,1)} %all-gather.6.cloned.1.call-done.all_ref, ...), custom_call_target="tpu_custom_call" | custom-call | flops 5905580032 | bytes 29527900 | tf_op jit(solution)/shard_map/front/pallas_call | solution.py:148
  63.5 11.3 %query.1 = (bf16[512,2048]{1,0:T(8,128)(2,1)}, bf16[512,2048]{1,0:T(8,128)(2,1)}) custom-call(bf16[512,2048]{1,0:T(8,128)(2,1)} %get-tuple-element.34.hid_ref, bf16[2048,2048]{1,0:T(8,128)(2,1)} %wq_ref.1, f32[1,256]{1,0:T(1,128)} %bitcast.30, f32[512,128]{1,0:T(8,128)} %get-tuple-element.111.cos_ref, f32[512,128]{1,0:T(8,128)} %get-tuple-element.110.sin_ref), custom_call_target="tpu_custom_call" | custom-call | flops 4294967296 | bytes 8388608 | tf_op jit(solution)/shard_map/query/pallas_call | solution.py:173
  74.8 15.5 %all-gather.8.cloned.1.call-done.k_ref.v_ref = bf16[4096,512]{1,0:T(8,128)(2,1)} async-done(((bf16[512,512]{1,0:T(8,128)(2,1)}), bf16[4096,512]{1,0:T(8,128)(2,1)}) %all-gather.8.cloned.1.call-update) | async-done | bytes 4194320 | tf_op jit(solution)/shard_map/all_gather | solution.py:434
  90.3 42.2 %attention.1 = (bf16[512,2048]{1,0:T(8,128)(2,1)}, f32[8,1,512]{2,1,0:T(1,128)}) custom-call(s32[1]{0:T(128)} %bitcast.rank_ref, bf16[512,2048]{1,0:T(8,128)(2,1)} %get-tuple-element.35.qs_ref, bf16[4096,512]{1,0:T(8,128)(2,1)} %all-gather.8.cloned.1.call-done.k_ref.v_ref, bf16[4096,512]{1,0:T(8,128)(2,1)} %all-gather.8.cloned.1.call-done.k_ref.v_ref, ...), custom_call_target="tpu_custom_call" | custom-call | flops 17179869184 | bytes 17179868 | tf_op jit(solution)/shard_map/attention/pallas_call | solution.py:258
  132.5 17.9 %post.1 = (bf16[512,2048]{1,0:T(8,128)(2,1)}, bf16[512,2048]{1,0:T(8,128)(2,1)}, bf16[512,2048]{1,0:T(8,128)(2,1)}, f32[1,2048]{1,0:T(1,128)}) custom-call(bf16[512,2048]{1,0:T(8,128)(2,1)} %get-tuple-element.37.o_ref, bf16[512,2048]{1,0:T(8,128)(2,1)} %get-tuple-element.38.merged_ref, bf16[512,2048]{1,0:T(8,128)(2,1)} %dy_ref.1, bf16[2048,2048]{1,0:T(8,128)(2,1)} %wo_ref.1, ...), custom_call_target="tpu_custom_call" | custom-call | flops 8589934592 | bytes 42949672 | tf_op jit(solution)/shard_map/post/pallas_call | solution.py:290
  150.4 66.5 %attention_back.1 = (bf16[512,2048]{1,0:T(8,128)(2,1)}, f32[1,256]{1,0:T(1,128)}, f32[4096,512]{1,0:T(8,128)}) custom-call(s32[1]{0:T(128)} %bitcast.rank_ref, bf16[512,2048]{1,0:T(8,128)(2,1)} %get-tuple-element.35.qs_ref, bf16[512,2048]{1,0:T(8,128)(2,1)} %get-tuple-element.40.do_ref, bf16[512,2048]{1,0:T(8,128)(2,1)} %get-tuple-element.37.o_ref, ...), custom_call_target="tpu_custom_call" | custom-call | flops 42949672960 | bytes 42949672 | tf_op jit(solution)/shard_map/attention_back/pallas_call | solution.py:384
  218.5 9.7 %fusion.37 = f32[2048,2048]{1,0:T(8,128)} fusion(bf16[512,2048]{1,0:T(8,128)(2,1)S(1)} %copy-done.1, bf16[512,2048]{1,0:T(8,128)(2,1)} %get-tuple-element.43), kind=kOutput, calls=%fused_computation.79 | convolution fusion | flops 4294967296 | bytes 20971520 | tf_op jit(solution)/shard_map/sd,sh->dh/dot_general | solution.py:442
  229.8 9.7 %fusion.38 = f32[2048,2048]{1,0:T(8,128)} fusion(bf16[512,2048]{1,0:T(8,128)(2,1)S(1)} %copy-done.17, bf16[512,2048]{1,0:T(8,128)(2,1)} %get-tuple-element.52), kind=kOutput, calls=%fused_computation.80 | convolution fusion | flops 4294967296 | bytes 20971520 | tf_op jit(solution)/shard_map/sh,sd->hd/dot_general | solution.py:438
  241.7 10.6 %fusion.36 = f32[512,2048]{1,0:T(8,128)} fusion(bf16[512,2048]{1,0:T(8,128)(2,1)} %get-tuple-element.43, bf16[2048,2048]{1,0:T(8,128)(2,1)} %wq_ref.1), kind=kOutput, calls=%fused_computation.78 | convolution fusion | flops 4294967296 | bytes 14680064 | tf_op jit(solution)/shard_map/sh,dh->sd/dot_general | solution.py:450
  252.3 12.9 %reduce-scatter.6.cloned.1.call-done = f32[512,512]{1,0:T(8,128)} async-done(((f32[4096,512]{1,0:T(8,128)}), f32[512,512]{1,0:T(8,128)}) %reduce-scatter.6.cloned.1.call-update) | async-done | bytes 1048592 | tf_op jit(solution)/shard_map/reduce_scatter | solution.py:409
  268.4 3.9 fusion.7
  272.3 3.3 fusion.22
  275.7 2.9 broadcast_select_fusion.1
  279.8 5.2 fusion.12
  285.1 12.4 %pad_maximum_fusion = f32[2048,1664]{0,1:T(8,128)} fusion(f32[2048,1152]{0,1:T(8,128)} %fusion.12, f32[2048,512]{0,1:T(8,128)} %fusion.22), kind=kLoop, calls=%fused_computation | loop fusion | flops 3407872 | bytes 27262976 | tf_op jit(solution)/shard_map/concatenate | solution.py:463
  299.1 10.2 %convolution_convert_fusion = bf16[2048,1152]{1,0:T(8,128)(2,1)} fusion(s32[512]{0:T(512)S(1)} %broadcast_select_fusion.6, bf16[1152,2048]{1,0:T(8,128)(2,1)} %wp_ref.1, bf16[512,2048]{1,0:T(8,128)(2,1)S(1)} %copy-done.6, pred[512]{0:T(512)(128)(4,1)S(1)} %fusion.27), kind=kOutput, calls=%fused_computation.1 | convolution fusion | flops 4836884480 | bytes 11536896 | tf_op jit(solution)/shard_map/sn,sc->nc/dot_general | solution.py:459
  309.4 46.8 %reduce-scatter.12.cloned.1.call-done = f32[256,2048]{1,0:T(8,128)} async-done(((f32[2048,2048]{1,0:T(8,128)}), f32[256,2048]{1,0:T(8,128)}) %reduce-scatter.12.cloned.1.call-update) | async-done | bytes 2097168 | tf_op jit(solution)/shard_map/reduce_scatter | solution.py:409
  356.2 2.7 convert_element_type.96
  359.0 87.8 %reduce-scatter.14.cloned.1.call-done = f32[256,2048]{1,0:T(8,128)} async-done(((f32[2048,2048]{1,0:T(8,128)}), f32[256,2048]{1,0:T(8,128)}) %reduce-scatter.14.cloned.1.call-update) | async-done | bytes 2097168 | tf_op jit(solution)/shard_map/reduce_scatter | solution.py:409
  446.8 2.7 convert_element_type.97
  449.6 72.8 %reduce-scatter.10.cloned.1.call-done = f32[256,1664]{0,1:T(8,128)} async-done(((f32[2048,1664]{0,1:T(8,128)}), f32[256,1664]{0,1:T(8,128)}) %reduce-scatter.10.cloned.1.call-update) | async-done | bytes 1703952 | tf_op jit(solution)/shard_map/reduce_scatter | solution.py:409
  524.9 36.7 %reduce-scatter.8.cloned.1.call-done.d_ref = bf16[256,1152]{1,0:T(8,128)(2,1)} async-done(((bf16[2048,1152]{1,0:T(8,128)(2,1)}), bf16[256,1152]{1,0:T(8,128)(2,1)}) %reduce-scatter.8.cloned.1.call-update) | async-done | bytes 589840 | tf_op jit(solution)/shard_map/reduce_scatter | solution.py:409
  561.7 7.2 unpool.1
  569.6 25.2 %psum.7 = bf16[5760]{0:T(1024)(128)(2,1)S(1)} all-reduce(f32[5760]{0:T(1024)S(1)} %constant_dynamic-update-slice_fusion), channel_id=1, replica_groups=mesh['dp'=4,'cp'=8] {'cp'}, use_global_device_ids=true, to_apply=%region_11.12 | all-reduce | flops 5760 | bytes 34560 | tf_op jit(solution)/shard_map/psum | solution.py:467
  596.5 13.1 %all-gather.12.cloned.1.call-done = bf16[2048,2048]{1,0:T(8,128)(2,1)} async-done(((bf16[256,2048]{1,0:T(8,128)(2,1)}), bf16[2048,2048]{1,0:T(8,128)(2,1)}) %all-gather.12.cloned.1.call-update) | async-done | bytes 8388624 | tf_op jit(solution)/shard_map/all_gather | solution.py:474
  609.6 48.8 %all-gather.14.cloned.1.call-done = bf16[2048,2048]{1,0:T(8,128)(2,1)} async-done(((bf16[256,2048]{1,0:T(8,128)(2,1)}), bf16[2048,2048]{1,0:T(8,128)(2,1)}) %all-gather.14.cloned.1.call-update) | async-done | bytes 8388624 | tf_op jit(solution)/shard_map/all_gather | solution.py:473
  658.4 46.4 %all-gather.10.cloned.1.call-done = bf16[2048,1664]{0,1:T(8,128)(2,1)} async-done(((bf16[256,1664]{0,1:T(8,128)(2,1)}), bf16[2048,1664]{0,1:T(8,128)(2,1)}) %all-gather.10.cloned.1.call-update) | async-done | bytes 6815760 | tf_op jit(solution)/shard_map/all_gather | solution.py:472
  709.1 5.2 slice_bitcast_fusion
  714.3 8.4 %copy.42 = bf16[2048,2048]{1,0:T(8,128)(2,1)} copy(bf16[2048,2048]{1,0:T(8,128)(2,1)} %all-gather.12.cloned.1.call-done) | data formatting | bytes 16777216
  722.7 8.4 %copy.43 = bf16[2048,2048]{1,0:T(8,128)(2,1)} copy(bf16[2048,2048]{1,0:T(8,128)(2,1)} %all-gather.14.cloned.1.call-done) | data formatting | bytes 16777216
  (98 shorter events, 28.6 us)
Async XLA Ops:
  7.2 40.1 %all-gather.6.cloned.1.call-start = ((), (), s32[]{:S(2)}) async-start(), calls=%async_computation.5 | async-start | bytes 5308416 | tf_op jit(solution)/shard_map/all_gather | solution.py:431
  8.5 6.5 copy-start.10
  8.5 7.6 %copy-start.7 = (bf16[2048]{0:T(1024)(128)(2,1)S(1)}, bf16[2048]{0:T(1024)(128)(2,1)}, u32[]{:S(2)}) copy-start(bf16[2048]{0:T(1024)(128)(2,1)} %param.20) | copy-start | bytes 12292
  8.5 8.2 %copy-start.15 = (bf16[256]{0:T(256)(128)(2,1)S(1)}, bf16[256]{0:T(256)(128)(2,1)}, u32[]{:S(2)}) copy-start(bf16[256]{0:T(256)(128)(2,1)} %param.25) | copy-start | bytes 1540
  15.0 75.4 %all-gather.8.cloned.1.call-start = ((), (), s32[]{:S(2)}) async-start(), calls=%async_computation.6 | async-start | bytes 4718592 | tf_op jit(solution)/shard_map/all_gather | solution.py:434
  47.3 14.4 %copy-start.14 = (bf16[256]{0:T(256)(128)(2,1)S(1)}, bf16[256]{0:T(256)(128)(2,1)}, u32[]{:S(2)}) copy-start(bf16[256]{0:T(256)(128)(2,1)} %param.24) | copy-start | bytes 1540
  47.3 15.0 %copy-start.9 = (bf16[2048]{0:T(1024)(128)(2,1)S(1)}, bf16[2048]{0:T(1024)(128)(2,1)}, u32[]{:S(2)}) copy-start(bf16[2048]{0:T(1024)(128)(2,1)} %param.27) | copy-start | bytes 12292
  61.4 203.8 %reduce-scatter.6.cloned.1.call-start = ((), (), s32[]{:S(2)}) async-start(), calls=%async_computation.7 | async-start | bytes 9437184 | tf_op jit(solution)/shard_map/reduce_scatter | solution.py:409
  216.9 1.6 copy-start.1
  217.0 139.2 %reduce-scatter.12.cloned.1.call-start = ((), (), s32[]{:S(2)}) async-start(), calls=%async_computation.11 | async-start | bytes 18874368 | tf_op jit(solution)/shard_map/reduce_scatter | solution.py:409
  228.2 1.6 copy-start.17
  228.3 218.5 %reduce-scatter.14.cloned.1.call-start = ((), (), s32[]{:S(2)}) async-start(), calls=%async_computation.13 | async-start | bytes 18874368 | tf_op jit(solution)/shard_map/reduce_scatter | solution.py:409
  239.5 0.9 copy-start.3
  239.5 1.7 copy-start
  239.6 282.9 %reduce-scatter.10.cloned.1.call-start = ((), (), s32[]{:S(2)}) async-start(), calls=%async_computation.9 | async-start | bytes 15335424 | tf_op jit(solution)/shard_map/reduce_scatter | solution.py:409
  252.3 16.1 %copy-start.12 = (bf16[2048,256]{1,0:T(8,128)(2,1)S(1)}, bf16[2048,256]{1,0:T(8,128)(2,1)}, u32[]{:S(2)}) copy-start(bf16[2048,256]{1,0:T(8,128)(2,1)} %wk_ref.1) | copy-start | bytes 3145732
  265.2 3.1 copy-start.13
  268.4 3.9 copy-start.2
  272.3 3.4 copy-start.4
  275.7 4.2 copy-start.16
  278.5 1.3 copy-start.5
  297.5 1.6 copy-start.6
  297.5 264.1 %reduce-scatter.8.cloned.1.call-start = ((), (), s32[]{:S(2)}) async-start(), calls=%async_computation.8 | async-start | bytes 5308416 | tf_op jit(solution)/shard_map/reduce_scatter | solution.py:409
  309.3 300.3 %all-gather.12.cloned.1.call-start = ((), (), s32[]{:S(2)}) async-start(), calls=%async_computation.12 | async-start | bytes 9437184 | tf_op jit(solution)/shard_map/all_gather | solution.py:474
  358.9 210.6 %copy-start.11 = (f32[1,256]{1,0:T(1,128)S(1)}, f32[1,256]{1,0:T(1,128)}, u32[]{:S(2)}) copy-start(f32[1,256]{1,0:T(1,128)} %get-tuple-element.49) | copy-start | bytes 3076
  358.9 210.7 %copy-start.8 = (f32[1,2048]{1,0:T(1,128)S(1)}, f32[1,2048]{1,0:T(1,128)}, u32[]{:S(2)}) copy-start(f32[1,2048]{1,0:T(1,128)} %get-tuple-element.50) | copy-start | bytes 24580
  359.0 299.4 %all-gather.14.cloned.1.call-start = ((), (), s32[]{:S(2)}) async-start(), calls=%async_computation.14 | async-start | bytes 9437184 | tf_op jit(solution)/shard_map/all_gather | solution.py:473
  449.6 255.2 %all-gather.10.cloned.1.call-start = ((), (), s32[]{:S(2)}) async-start(), calls=%async_computation.10 | async-start | bytes 7667712 | tf_op jit(solution)/shard_map/all_gather | solution.py:472
Sparse Core Ops, SparseCore 0:
  15.1 32.1 all-gather.5
  61.5 28.7 all-gather.7
  217.1 48.0 reduce-scatter.5
  267.4 88.6 reduce-scatter.11
  358.4 88.3 reduce-scatter.13
  449.0 73.4 reduce-scatter.9
  525.3 36.2 reduce-scatter.7
  563.9 45.6 all-gather.11
  611.8 46.5 all-gather.13
  660.4 44.3 all-gather.9
